TPU v7x, 512 devices: a whole 4x4x16 slice. The times are simulated.
512 devices in a mesh: gx: 16 (over z), gy: 8 (over y, core), gz: 4 (over x).
Axes of the slice: x: 4, y: 4, z: 16, core: 2. Of those that a mesh axis runs over, the one named last changes fastest.
Arguments:
- displace: float32 [3, 64, 128, 512], P(None, 'gx', 'gy', 'gz'), may hold values from -4 to 4
- dir_a: float32 [3, 64, 128, 512], P(None, 'gx', 'gy', 'gz'), may hold values from -6 to 6
- dir_b: float32 [3, 64, 128, 512], P(None, 'gx', 'gy', 'gz'), may hold values from -6 to 6
- force: float32 [3, 64, 128, 512], P(None, 'gx', 'gy', 'gz'), may hold values from -6 to 6
- damage: float32 [64, 128, 512], P('gx', 'gy', 'gz'), may hold values from 0 to 0.9
- slip: float32 [12, 64, 128, 512], P(None, 'gx', 'gy', 'gz'), may hold values from -2 to 2
- resist: float32 [12, 64, 128, 512], P(None, 'gx', 'gy', 'gz'), may hold values from 0.5 to 2
- grains: int32 [64, 128, 512], P('gx', 'gy', 'gz'), may hold values from 0 to 63
- counts: int32 [64, 64, 4], P('gx', 'gy', 'gz'), may hold values from 8 to 40, as said below
- schmid_raw: float32 [64, 12, 9], replicated, may hold values from -3 to 3
Outputs:
- residual: float32 [3, 64, 128, 512], P(None, 'gx', 'gy', 'gz')
- tangent_a: float32 [3, 64, 128, 512], P(None, 'gx', 'gy', 'gz')
- tangent_b: float32 [3, 64, 128, 512], P(None, 'gx', 'gy', 'gz')
- slip_new: float32 [12, 64, 128, 512], P(None, 'gx', 'gy', 'gz')
- resist_new: float32 [12, 64, 128, 512], P(None, 'gx', 'gy', 'gz')
Inputs may be any that keep to these rules, and one draw needn't show every extreme that they name: `counts`: each block is 2 x 128 points of one first-dimension index; heavy blocks form a band in the second dimension whose place changes with the third-dimension block.
All inputs are finite; a program needn't handle non-finite values.
Results may differ from a plain program's by a relative error of at most 0.0003.
Values sent between devices are 32-bit elements; how exact they have to be, the bound alone decides.
No kernel may reach another device: no remote copies, remote signals or barrier semaphores. Data moves between devices by JAX's collectives and lax.ppermute only.
A program may use at most 64 MiB of HBM per device.

v0:
```python
import math

import jax
import jax.numpy as jnp
from jax import lax
from jax.experimental import pallas as pl
from jax.experimental.pallas import tpu as pltpu
from jax.sharding import PartitionSpec as P

SLIP = 12
GRAINS = 64
DEV = 5
WIDE = 2
UNROLL = 4
NAMES = ("xlo", "xhi", "yeven", "yodd", "zlo", "zhi")
ORDER_FIRST = ("xlo", "xhi", "yeven", "yodd", "zlo", "zhi")
ORDER_LAST = ("yeven", "xlo", "xhi", "zlo", "zhi", "yodd")
UNROLL_MASKED = 2
LANES = 128
VMEM_LIMIT = 12 * 1024 * 1024


lame_first = 0.8
rate_scale = 1.5
harden_rate = 0.3
floor_stiff = 0.05

RT2 = math.sqrt(2.0)
RT6 = math.sqrt(6.0)


def entries(system):
    return range(min(system + 1, DEV))


SLOTS = [(a, c) for a in range(SLIP) for c in entries(a)]
SLOT_OF = {pair: k for k, pair in enumerate(SLOTS)}


def total(terms):
    terms = list(terms)
    while len(terms) > 1:
        terms = [terms[i] + terms[i + 1] if i + 1 < len(terms) else terms[i] for i in range(0, len(terms), 2)]
    return terms[0]


def chain(terms):
    terms = list(terms)
    acc = terms[0]
    for term in terms[1:]:
        acc = acc + term
    return acc


def pack_lane(tiles, lane):
    at = lax.broadcasted_iota(jnp.int32, (8, LANES), 1)
    packed = jnp.zeros((8, LANES), jnp.float32)
    for k, tile in enumerate(tiles):
        shift = (k - lane) % LANES
        moved = pltpu.roll(tile, shift, 1) if shift else tile
        packed = jnp.where(at == k, moved, packed)
    return packed


def parity():
    return lax.rem(lax.axis_index("gy"), 2)


def in_order(refs, order):
    return [refs[order.index(name)] for name in NAMES]


def faces_kernel(u_hbm, a_hbm, b_hbm, fields, *refs):
    xlo, xhi, yeven, yodd, zlo, zhi = in_order(refs[:6], ORDER_FIRST)
    sem = refs[6]
    nx, ny = fields.shape[1], fields.shape[2]
    odd = parity()
    row_even, row_odd = (1 - odd) * (ny - 1), odd * (ny - 1)
    copies = [
        pltpu.make_async_copy(ref, fields.at[pl.ds(3 * f, 3)], sem.at[f]) for f, ref in enumerate((u_hbm, a_hbm, b_hbm))
    ]
    for copy in copies:
        copy.start()
    tiles = []
    for n in range(9):
        if n % 3 == 0:
            copies[n // 3].wait()
        xlo[n] = fields[n, 0]
        xhi[n] = fields[n, nx - 1]
        for x in range(nx):
            row = n * nx + x
            yeven[pl.ds(row, 1), :] = fields[n, x, pl.ds(row_even, 1), :]
            yodd[pl.ds(row, 1), :] = fields[n, x, pl.ds(row_odd, 1), :]
            for h in range(ny // 8):
                tiles.append(fields[n, x, pl.ds(8 * h, 8), :])
    zlo[...] = pack_lane(tiles, 0)
    zhi[...] = pack_lane(tiles, LANES - 1)


def tile_counts(count_ref, x, h):
    row_at = lax.broadcasted_iota(jnp.int32, (8, LANES), 0)
    numbers = [count_ref[x, 0, 4 * h + j] for j in range(4)]
    upper = jnp.where(row_at < 2, numbers[0], numbers[1])
    lower = jnp.where(row_at < 6, numbers[2], numbers[3])
    return jnp.where(row_at < 4, upper, lower)


def stiffness(damage):
    undamaged = 1.0 - damage
    return undamaged * undamaged + floor_stiff


def table_kernel(raw_hbm, *refs):
    sources, count_hbm, (rows_ref, turn_ref, past_ref, steps_ref) = refs[:4], refs[4], refs[5:9]
    targets, count_out, raw_ref, wide_ref, count_ref, sem = refs[9:13], refs[13], refs[14], refs[15], refs[16], refs[17]
    _, slip_ref, _, grain_ref = targets
    numbers = [
        pltpu.make_async_copy(count_hbm, count_ref, sem.at[5]),
        pltpu.make_async_copy(count_hbm, count_out, sem.at[6]),
    ]
    for copy in numbers:
        copy.start()
    nx, ny = grain_ref.shape[0], grain_ref.shape[1]
    first = pltpu.make_async_copy(raw_hbm, raw_ref, sem.at[4])
    first.start()
    copies = [pltpu.make_async_copy(source, target, sem.at[k]) for k, (source, target) in enumerate(zip(sources, targets))]
    for copy in copies:
        copy.start()
    wide_ref[...] = jnp.zeros_like(wide_ref)
    first.wait()
    wide_ref[:, pl.ds(0, SLIP), pl.ds(0, GRAINS)] = raw_ref[...]
    comp = [wide_ref[i] for i in range(9)]
    base = [
        (comp[0] - comp[4]) * (1.0 / RT2),
        (2.0 * comp[8] - comp[0] - comp[4]) * (1.0 / RT6),
        (comp[1] + comp[3]) * (1.0 / RT2),
        (comp[2] + comp[6]) * (1.0 / RT2),
        (comp[5] + comp[7]) * (1.0 / RT2),
    ]
    row_at = lax.broadcasted_iota(jnp.int32, (24, LANES), 0)
    both = []
    for c in range(DEV):
        both.append(jnp.where(row_at == 16 + c, 1.0, base[c]))
    for k in range(DEV - 1):
        for j in range(k + 1, DEV):
            first, second = both[k][k : k + 1], both[j][k : k + 1]
            square = first * first + second * second
            good = square > 0.0
            scale = lax.rsqrt(jnp.where(good, square, 1.0))
            cosine = jnp.where(good, first * scale, 1.0)
            sine = jnp.where(good, second * scale, 0.0)
            both[k], both[j] = cosine * both[k] + sine * both[j], cosine * both[j] - sine * both[k]
    for copy in copies + numbers:
        copy.wait()
    for x in range(nx):
        for h in range(ny // 8):
            rows = pl.ds(8 * h, 8)
            ids = grain_ref[x, rows, :]

            def look(row):
                spread = jnp.broadcast_to(row, (8, LANES))
                return jnp.take_along_axis(spread, ids, axis=1, mode="promise_in_bounds")

            steps_ref[x, rows, :] = tile_counts(count_ref, x, h)
            past = [None] * DEV
            for k, (a, c) in enumerate(SLOTS):
                value = look(both[c][a : a + 1])
                rows_ref[k, x, rows, :] = value
                term = slip_ref[a, x, rows, :] * value
                past[c] = term if past[c] is None else past[c] + term
            for c in range(DEV):
                past_ref[c, x, rows, :] = past[c]
            for c in range(DEV):
                for d in range(DEV):
                    turn_ref[DEV * c + d, x, rows, :] = look(both[c][16 + d : 17 + d])


def sort_halos(odd, yeven, yodd, ylo, yhi):
    upper = odd == 0
    yhi[...] = jnp.where(upper, yeven[...], yodd[...])
    ylo[...] = jnp.where(upper, yodd[...], yeven[...])


def gradient_parts(field, halos, f, x, h):
    xlo, xhi, ylo, yhi, zlo, zhi = halos
    nx, ny = field.shape[1], field.shape[2]
    row_at = lax.broadcasted_iota(jnp.int32, (8, LANES), 0)
    lane_at = lax.broadcasted_iota(jnp.int32, (8, LANES), 1)
    out = []
    for c in range(3):
        n = 3 * f + c
        here = field[n, x, pl.ds(8 * h, 8), :]
        ahead = field[n, x + 1, pl.ds(8 * h, 8), :] if x + 1 < nx else xhi[n, pl.ds(8 * h, 8), :]
        behind = field[n, x - 1, pl.ds(8 * h, 8), :] if x > 0 else xlo[n, pl.ds(8 * h, 8), :]
        row = n * nx + x
        if 8 * h + 8 < ny:
            over = field[n, x, pl.ds(8 * h + 1, 8), :]
        else:
            edge = jnp.broadcast_to(yhi[pl.ds(row, 1), :], (8, LANES))
            over = jnp.where(row_at == 7, edge, pltpu.roll(here, 7, 0))
        if h > 0:
            under = field[n, x, pl.ds(8 * h - 1, 8), :]
        else:
            edge = jnp.broadcast_to(ylo[pl.ds(row, 1), :], (8, LANES))
            under = jnp.where(row_at == 0, edge, pltpu.roll(here, 1, 0))
        k = row * (ny // 8) + h
        top = pltpu.roll(zhi[...], (LANES - 1 - k) % LANES, 1)
        low = pltpu.roll(zlo[...], (LANES - k) % LANES, 1)
        right = jnp.where(lane_at == LANES - 1, top, pltpu.roll(here, LANES - 1, 1))
        left = jnp.where(lane_at == 0, low, pltpu.roll(here, 1, 1))
        out.append((ahead - behind, over - under, right - left))
    return out


def strain_parts(field, halos, f, x0, h):
    per = []
    for x in range(x0, x0 + WIDE):
        g = gradient_parts(field, halos, f, x, h)
        trace = (g[0][0] + g[1][1] + g[2][2]) * 0.5
        per.append(
            (
                trace,
                (g[0][0] - g[1][1]) * (0.5 / RT2),
                (2.0 * g[2][2] - g[0][0] - g[1][1]) * (0.5 / RT6),
                (g[0][1] + g[1][0]) * (0.5 / RT2),
                (g[0][2] + g[2][0]) * (0.5 / RT2),
                (g[1][2] + g[2][1]) * (0.5 / RT2),
            )
        )
    stacked = [jnp.stack([p[i] for p in per], 0) for i in range(6)]
    return stacked[0], stacked[1:]


def full_tensor(mean, dev):
    side = dev[1] * (1.0 / RT6)
    return [
        mean - side + dev[0] * (1.0 / RT2),
        mean - side - dev[0] * (1.0 / RT2),
        mean + dev[1] * (2.0 / RT6),
        dev[2] * (1.0 / RT2),
        dev[3] * (1.0 / RT2),
        dev[4] * (1.0 / RT2),
    ]


SYM = ((0, 3, 4), (3, 1, 5), (4, 5, 2))


def several(step, first, number):
    def body(turn, state):
        for k in range(number):
            state = step(first + number * turn + k, state)
        return state

    return body


def material_kernel(
    count_vmem, fields, xlo, xhi, yeven, yodd, zlo, zhi, damage_ref, slip_ref, resist_ref, rows_ref, turn_ref,
    past_ref, steps_ref,
    slip_hbm, resist_hbm, tensor_out, out0, out1, out2, out3, out4, out5,
    ylo, yhi, scaled_ref, sums_ref, soft_ref, slip_out, resist_out, count_ref, sent, told,
):
    nx, ny = fields.shape[1], fields.shape[2]
    odd = parity()
    row_even, row_odd = (1 - odd) * (ny - 1), odd * (ny - 1)
    oxlo, oxhi, oyeven, oyodd, ozlo, ozhi = in_order((out0, out1, out2, out3, out4, out5), ORDER_LAST)
    tell = pltpu.make_async_copy(count_vmem, count_ref, told)
    tell.start()
    sort_halos(odd, yeven, yodd, ylo, yhi)
    halos = (xlo, xhi, ylo, yhi, zlo, zhi)
    copies = []
    for x0 in range(0, nx, WIDE):
        for h in range(ny // 8):
            spot = (pl.ds(x0, WIDE), pl.ds(8 * h, 8), slice(None))
            steps = steps_ref[spot]
            count = steps.astype(jnp.float32)
            time_step = 1.0 / count
            degrade = stiffness(damage_ref[spot])
            scale = jnp.sqrt(rate_scale * degrade * time_step)
            for k in range(len(SLOTS)):
                scaled_ref[k] = rows_ref[(k,) + spot] * scale

            def entry(a, c):
                return scaled_ref[SLOT_OF[(a, c)]]

            def turned(vector):
                return [total(turn_ref[(DEV * c + d,) + spot] * vector[d] for d in range(DEV)) for c in range(DEV)]

            def returned(vector):
                return [total(turn_ref[(DEV * c + d,) + spot] * vector[c] for c in range(DEV)) for d in range(DEV)]

            def project(vector, a):
                return total(entry(a, c) * vector[c] for c in entries(a))

            def gather(weights, c):
                return chain(entry(a, c) * weights[a] for a in range(SLIP) if c in entries(a))

            trace_u, strain = strain_parts(fields, halos, 0, x0, h)
            strain = turned(strain)
            lift = jnp.sqrt(degrade * count * (1.0 / rate_scale))
            drive = tuple(lift * (strain[c] - past_ref[(c,) + spot]) for c in range(DEV))
            grow = (rate_scale * harden_rate) * time_step
            zero = jnp.zeros_like(count)

            def rates(driving, growth):
                return [jnp.tanh(project(driving, a) / (resist_ref[(a,) + spot] + growth)) for a in range(SLIP)]

            def substep(_, state):
                driving, growth = state
                rate = rates(driving, growth)
                for a in range(SLIP):
                    sums_ref[a] = sums_ref[a] + rate[a]
                growth = growth + grow * total(jnp.abs(r) for r in rate)
                driving = tuple(driving[c] - gather(rate, c) for c in range(DEV))
                return driving, growth

            def masked(turn, state):
                driving, growth = state
                live = turn < steps
                return substep(turn, (tuple(jnp.where(live, d, 0.0) for d in driving), growth))

            for a in range(SLIP):
                sums_ref[a] = zero
            if x0 == 0 and h == 0:
                tell.wait()
            least = most = count_ref[x0, 0, 4 * h]
            for x in range(x0, x0 + WIDE):
                for j in range(4):
                    least = jnp.minimum(least, count_ref[x, 0, 4 * h + j])
                    most = jnp.maximum(most, count_ref[x, 0, 4 * h + j])
            full = lax.div(least, UNROLL)
            state = lax.fori_loop(0, full, several(substep, 0, UNROLL), (drive, zero))
            first = UNROLL * full
            rest = lax.div(most - first + (UNROLL_MASKED - 1), UNROLL_MASKED)
            _, growth = lax.fori_loop(0, rest, several(masked, first, UNROLL_MASKED), state)
            sums = [sums_ref[a] for a in range(SLIP)]
            for a in range(SLIP):
                slip_out[(a,) + spot] = slip_ref[(a,) + spot] + (rate_scale * time_step) * sums[a]
                resist_out[(a,) + spot] = resist_ref[(a,) + spot] + growth
            group = x0 // WIDE * (ny // 8) + h
            for kind, (held, away) in enumerate(((slip_out, slip_hbm), (resist_out, resist_hbm))):
                part = (slice(None),) + spot
                copy = pltpu.make_async_copy(held.at[part], away.at[part], sent.at[kind, group])
                copy.start()
                copies.append(copy)
            drive = [drive[c] - gather(sums, c) for c in range(DEV)]
            stress = returned([scale * d for d in drive])
            for a, ratio in enumerate(rates(drive, growth)):
                soft_ref[a] = (1.0 - ratio * ratio) / (resist_ref[(a,) + spot] + growth)
            bulk = degrade * (lame_first + 1.0 / 3.0)
            for k, value in enumerate(full_tensor(bulk * trace_u, stress)):
                tensor_out[(k,) + spot] = value

            def tangent(f):
                trace_v, dev = strain_parts(fields, halos, f, x0, h)
                dev = [degrade * d for d in dev]
                local = turned(dev)
                weights = [soft_ref[a] * project(local, a) for a in range(SLIP)]
                loss = returned([count * gather(weights, c) for c in range(DEV)])
                for k, value in enumerate(full_tensor(bulk * trace_v, [d - q for d, q in zip(dev, loss)])):
                    tensor_out[(6 * f + k,) + spot] = value
                return 0

            tangent(1)
            tangent(2)
    tiles = []
    for f in range(3):
        for i in range(3):
            n = 3 * f + i
            sx, sy, sz = (6 * f + SYM[i][j] for j in range(3))
            oxlo[n] = tensor_out[sx, 0]
            oxhi[n] = tensor_out[sx, nx - 1]
            for x in range(nx):
                oyeven[pl.ds(n * nx + x, 1), :] = tensor_out[sy, x, pl.ds(row_even, 1), :]
                oyodd[pl.ds(n * nx + x, 1), :] = tensor_out[sy, x, pl.ds(row_odd, 1), :]
                for h in range(ny // 8):
                    tiles.append(tensor_out[sz, x, pl.ds(8 * h, 8), :])
    ozlo[...] = pack_lane(tiles, 0)
    ozhi[...] = pack_lane(tiles, LANES - 1)
    for copy in copies:
        copy.wait()


def diverge_kernel(
    tensor_ref, xlo, xhi, yeven, yodd, zlo, zhi, force_ref, residual, tangent_a, tangent_b, ylo, yhi
):
    nx, ny = tensor_ref.shape[1], tensor_ref.shape[2]
    sort_halos(parity(), yeven, yodd, ylo, yhi)
    row_at = lax.broadcasted_iota(jnp.int32, (8, LANES), 0)
    lane_at = lax.broadcasted_iota(jnp.int32, (8, LANES), 1)
    for f, out in enumerate((residual, tangent_a, tangent_b)):
        for i in range(3):
            n = 3 * f + i
            sx, sy, sz = (6 * f + SYM[i][j] for j in range(3))
            for x in range(nx):
                for h in range(ny // 8):
                    rows = pl.ds(8 * h, 8)
                    ahead = tensor_ref[sx, x + 1, rows, :] if x + 1 < nx else xhi[n, rows, :]
                    behind = tensor_ref[sx, x - 1, rows, :] if x > 0 else xlo[n, rows, :]
                    row = n * nx + x
                    here = tensor_ref[sy, x, rows, :]
                    if 8 * h + 8 < ny:
                        over = tensor_ref[sy, x, pl.ds(8 * h + 1, 8), :]
                    else:
                        edge = jnp.broadcast_to(yhi[pl.ds(row, 1), :], (8, LANES))
                        over = jnp.where(row_at == 7, edge, pltpu.roll(here, 7, 0))
                    if h > 0:
                        under = tensor_ref[sy, x, pl.ds(8 * h - 1, 8), :]
                    else:
                        edge = jnp.broadcast_to(ylo[pl.ds(row, 1), :], (8, LANES))
                        under = jnp.where(row_at == 0, edge, pltpu.roll(here, 1, 0))
                    k = row * (ny // 8) + h
                    here = tensor_ref[sz, x, rows, :]
                    top = pltpu.roll(zhi[...], (LANES - 1 - k) % LANES, 1)
                    low = pltpu.roll(zlo[...], (LANES - k) % LANES, 1) if k else zlo[...]
                    right = jnp.where(lane_at == LANES - 1, top, pltpu.roll(here, LANES - 1, 1))
                    left = jnp.where(lane_at == 0, low, pltpu.roll(here, 1, 1))
                    value = 0.5 * ((ahead - behind) + (over - under) + (right - left))
                    if f == 0:
                        value = value + force_ref[i, x, rows, :]
                    out[i, x, rows, :] = value


def exchange(faces, order):
    def shift(value, axis, step):
        size = lax.axis_size(axis)
        return lax.ppermute(value, axis, [(i, i + step) for i in range(size) if 0 <= i + step < size])

    def swap(value, axis, first):
        size = lax.axis_size(axis)
        pairs = [(i, i + 1) for i in range(first, size - 1, 2)]
        return lax.ppermute(value, axis, pairs + [(j, i) for i, j in pairs])

    moves = {
        "xlo": lambda v: ("xhi", shift(v, "gx", -1)),
        "xhi": lambda v: ("xlo", shift(v, "gx", 1)),
        "yeven": lambda v: ("yeven", swap(v, "gy", 0)),
        "yodd": lambda v: ("yodd", swap(v, "gy", 1)),
        "zlo": lambda v: ("zhi", shift(v, "gz", -1)),
        "zhi": lambda v: ("zlo", shift(v, "gz", 1)),
    }
    got = {}
    for name, value in zip(order, faces):
        side, value = moves[name](value)
        got[side] = value
    return [got[name] for name in NAMES]


def in_hbm(value):
    return pltpu.with_memory_space_constraint(value, pltpu.HBM)


def shaped(*dims):
    return jax.ShapeDtypeStruct(dims, jnp.float32)


def on_device(displace, dir_a, dir_b, force, damage, slip, resist, grains, counts, schmid_raw):
    nx, ny, nz = damage.shape
    shape_of = {"x": shaped(9, ny, nz), "y": shaped(9 * nx, nz), "z": shaped(8, nz)}
    vmem = pl.BlockSpec(memory_space=pltpu.VMEM)
    hbm = pl.BlockSpec(memory_space=pltpu.HBM)
    params = pltpu.CompilerParams(vmem_limit_bytes=VMEM_LIMIT)
    fields, *faces = pl.pallas_call(
        faces_kernel,
        out_shape=[shaped(9, nx, ny, nz)] + [shape_of[name[0]] for name in ORDER_FIRST],
        in_specs=[hbm] * 3,
        out_specs=[vmem] * 7,
        scratch_shapes=[pltpu.SemaphoreType.DMA((3,))],
        compiler_params=params,
        name="faces",
    )(*(in_hbm(v) for v in (displace, dir_a, dir_b)))
    points = [in_hbm(v) for v in (damage, slip, resist, grains)]
    number = jnp.transpose(counts, (0, 2, 1))
    rows, turn, past, steps, *points, number = pl.pallas_call(
        table_kernel,
        out_shape=[shaped(k, nx, ny, nz) for k in (len(SLOTS), DEV * DEV, DEV)]
        + [jax.ShapeDtypeStruct((nx, ny, nz), jnp.int32)]
        + [jax.ShapeDtypeStruct(p.shape, p.dtype) for p in points]
        + [jax.ShapeDtypeStruct(number.shape, number.dtype)],
        in_specs=[hbm] * 6,
        out_specs=[vmem] * 9,
        scratch_shapes=[
            pltpu.VMEM((9, SLIP, GRAINS), jnp.float32),
            pltpu.VMEM((9, 24, LANES), jnp.float32),
            pltpu.SMEM(number.shape, jnp.int32),
            pltpu.SemaphoreType.DMA((7,)),
        ],
        compiler_params=params,
        name="table",
    )(in_hbm(jnp.transpose(schmid_raw, (2, 1, 0))), *points, in_hbm(number))
    halos = exchange(faces, ORDER_FIRST)
    groups = nx // WIDE * (ny // 8)
    outs = pl.pallas_call(
        material_kernel,
        out_shape=[shaped(SLIP, nx, ny, nz)] * 2 + [shaped(18, nx, ny, nz)]
        + [shape_of[name[0]] for name in ORDER_LAST],
        in_specs=[vmem] * 15,
        out_specs=[hbm] * 2 + [vmem] * 7,
        scratch_shapes=[
            pltpu.VMEM((9 * nx, nz), jnp.float32),
            pltpu.VMEM((9 * nx, nz), jnp.float32),
            pltpu.VMEM((len(SLOTS), WIDE, 8, LANES), jnp.float32),
            pltpu.VMEM((SLIP, WIDE, 8, LANES), jnp.float32),
            pltpu.VMEM((SLIP, WIDE, 8, LANES), jnp.float32),
            pltpu.VMEM((SLIP, nx, ny, nz), jnp.float32),
            pltpu.VMEM((SLIP, nx, ny, nz), jnp.float32),
            pltpu.SMEM(number.shape, jnp.int32),
            pltpu.SemaphoreType.DMA((2, groups)),
            pltpu.SemaphoreType.DMA,
        ],
        compiler_params=params,
        name="material",
    )(number, fields, *halos, *points[:3], rows, turn, past, steps)
    slip_new, resist_new, tensors = outs[:3]
    halos = exchange(outs[3:], ORDER_LAST)
    residual, tangent_a, tangent_b = pl.pallas_call(
        diverge_kernel,
        out_shape=[shaped(3, nx, ny, nz)] * 3,
        in_specs=[vmem] * 8,
        out_specs=[vmem] * 3,
        scratch_shapes=[pltpu.VMEM((9 * nx, nz), jnp.float32)] * 2,
        compiler_params=params,
        name="diverge",
    )(tensors, *halos, force)
    return residual, tangent_a, tangent_b, slip_new, resist_new


def solution(mesh):
    field = P(None, "gx", "gy", "gz")
    point = P("gx", "gy", "gz")
    return jax.shard_map(
        on_device,
        mesh=mesh,
        in_specs=(field, field, field, field, point, field, field, point, point, P()),
        out_specs=(field,) * 5,
        check_vma=False,
    )
```

profile of v0, /device:TPU:282, one launch (start us, length us, event | category | flops | bytes accessed | tf_op | source)
XLA Modules:
  0.0 59.7 jit_solution(13108470124065159560)
XLA Ops:
  0.6 1.2 %faces.1 = (f32[9,4,16,128]{3,2,1,0:T(8,128)S(1)}, f32[9,16,128]{2,1,0:T(8,128)S(1)}, f32[9,16,128]{2,1,0:T(8,128)S(1)}, f32[36,128]{1,0:T(8,128)S(1)}, f32[36,1...) custom-call(f32[3,4,16,128]{3,2,1,0:T(8,128)} %u_hbm.1, f32[3,4,16,128]{3,2,1,0:T(8,128)} %a_hbm.1, ...), custom_call_target="tpu_custom_call" | custom-call | tf_op jit(solution)/shard_map/faces/pallas_call | solution.py:464
  1.9 2.9 %collective-permute-start = (f32[9,16,128]{2,1,0:T(8,128)S(1)}, f32[9,16,128]{2,1,0:T(8,128)S(1)}, u32[]{:S(2)}, u32[]{:S(2)}) collective-permute-start(f32[9,16,128]{2,1,0:T(8,128)S(1)} %get-tuple-element.34), channel_id=1, source_target_pairs={{0,32},{32,64},{64,96},{96,128},{128,160},{160,192},{192,224},{224... | collective-permute-start | bytes 221192 | tf_op jit(solution)/shard_map/ppermute | solution.py:428
  4.8 4.1 %collective-permute-start.1 = (f32[9,16,128]{2,1,0:T(8,128)S(1)}, f32[9,16,128]{2,1,0:T(8,128)S(1)}, u32[]{:S(2)}, u32[]{:S(2)}) collective-permute-start(f32[9,16,128]{2,1,0:T(8,128)S(1)} %get-tuple-element.35), channel_id=1, source_target_pairs={{32,0},{64,32},{96,64},{128,96},{160,128},{192,160},{224,192},{256... | collective-permute-start | bytes 221192 | tf_op jit(solution)/shard_map/ppermute | solution.py:428
  8.9 1.9 %collective-permute-start.2 = (f32[36,128]{1,0:T(8,128)S(1)}, f32[36,128]{1,0:T(8,128)S(1)}, u32[]{:S(2)}, u32[]{:S(2)}) collective-permute-start(f32[36,128]{1,0:T(8,128)S(1)} %get-tuple-element.36), channel_id=1, source_target_pairs={{0,4},{8,12},{16,20},{24,28},{4,0},{12,8},{20,16},{28,24},{1,5},{9... | collective-permute-start | bytes 55304 | tf_op jit(solution)/shard_map/ppermute | solution.py:433
  10.9 2.8 %collective-permute-start.3 = (f32[36,128]{1,0:T(8,128)S(1)}, f32[36,128]{1,0:T(8,128)S(1)}, u32[]{:S(2)}, u32[]{:S(2)}) collective-permute-start(f32[36,128]{1,0:T(8,128)S(1)} %get-tuple-element.37), channel_id=1, source_target_pairs={{4,8},{12,16},{20,24},{8,4},{16,12},{24,20},{5,9},{13,17},{21,25},... | collective-permute-start | bytes 55304 | tf_op jit(solution)/shard_map/ppermute | solution.py:433
  13.6 3.4 %collective-permute-start.4 = (f32[8,128]{1,0:T(8,128)S(1)}, f32[8,128]{1,0:T(8,128)S(1)}, u32[]{:S(2)}, u32[]{:S(2)}) collective-permute-start(f32[8,128]{1,0:T(8,128)S(1)} %get-tuple-element.38), channel_id=1, source_target_pairs={{0,1},{1,2},{2,3},{4,5},{5,6},{6,7},{8,9},{9,10},{10,11},{12,13},{... | collective-permute-start | bytes 12296 | tf_op jit(solution)/shard_map/ppermute | solution.py:428
  17.0 2.1 %collective-permute-done.4.zlo = f32[8,128]{1,0:T(8,128)S(1)} collective-permute-done((f32[8,128]{1,0:T(8,128)S(1)}, f32[8,128]{1,0:T(8,128)S(1)}, u32[]{:S(2)}, u32[]{:S(2)}) %collective-permute-start.4) | collective-permute-done | bytes 4128 | tf_op jit(solution)/shard_map/ppermute | solution.py:428
  19.1 1.9 %collective-permute-start.5 = (f32[8,128]{1,0:T(8,128)S(1)}, f32[8,128]{1,0:T(8,128)S(1)}, u32[]{:S(2)}, u32[]{:S(2)}) collective-permute-start(f32[8,128]{1,0:T(8,128)S(1)} %get-tuple-element.39), channel_id=1, source_target_pairs={{1,0},{2,1},{3,2},{5,4},{6,5},{7,6},{9,8},{10,9},{11,10},{13,12},{... | collective-permute-start | bytes 12296 | tf_op jit(solution)/shard_map/ppermute | solution.py:428
  21.1 2.0 %table.1 = (f32[50,4,16,128]{3,2,1,0:T(8,128)S(1)}, f32[25,4,16,128]{3,2,1,0:T(8,128)S(1)}, f32[5,4,16,128]{3,2,1,0:T(8,128)S(1)}, s32[4,16,128]{2,1,0:T(8,128)S...) custom-call(f32[9,12,64]{2,1,0:T(8,128)} %bitcast.4, ...), custom_call_target="tpu_custom_call" | custom-call | tf_op jit(solution)/shard_map/table/pallas_call | solution.py:475
  23.0 1.6 %collective-permute-done.5.zhi = f32[8,128]{1,0:T(8,128)S(1)} collective-permute-done((f32[8,128]{1,0:T(8,128)S(1)}, f32[8,128]{1,0:T(8,128)S(1)}, u32[]{:S(2)}, u32[]{:S(2)}) %collective-permute-start.5) | collective-permute-done | bytes 4128 | tf_op jit(solution)/shard_map/ppermute | solution.py:428
  24.6 0.0 collective-permute-done.2.yeven
  24.6 0.0 collective-permute-done.3.yodd
  24.6 0.0 collective-permute-done.xlo
  24.6 0.0 collective-permute-done.1.xhi
  24.6 0.0 copy-start
  24.7 6.8 %material.1 = (f32[12,4,16,128]{3,2,1,0:T(8,128)}, f32[12,4,16,128]{3,2,1,0:T(8,128)}, f32[18,4,16,128]{3,2,1,0:T(8,128)S(1)}, f32[36,128]{1,0:T(8,128)S(1)}, f3...) custom-call(s32[4,1,8]{2,1,0:T(1,128)S(1)} %get-tuple-element.32.cou, ...), custom_call_target="tpu_custom_call" | custom-call | tf_op jit(solution)/shard_map/material/pallas_call | solution.py:494
  31.5 1.9 %collective-permute-start.6 = (f32[9,16,128]{2,1,0:T(8,128)S(1)}, f32[9,16,128]{2,1,0:T(8,128)S(1)}, u32[]{:S(2)}, u32[]{:S(2)}) collective-permute-start(f32[9,16,128]{2,1,0:T(8,128)S(1)} %get-tuple-element.48), channel_id=1, source_target_pairs={{0,32},{32,64},{64,96},{96,128},{128,160},{160,192},{192,224},{224... | collective-permute-start | bytes 221192 | tf_op jit(solution)/shard_map/ppermute | solution.py:428
  33.4 5.1 %collective-permute-start.7 = (f32[9,16,128]{2,1,0:T(8,128)S(1)}, f32[9,16,128]{2,1,0:T(8,128)S(1)}, u32[]{:S(2)}, u32[]{:S(2)}) collective-permute-start(f32[9,16,128]{2,1,0:T(8,128)S(1)} %get-tuple-element.49), channel_id=1, source_target_pairs={{32,0},{64,32},{96,64},{128,96},{160,128},{192,160},{224,192},{256... | collective-permute-start | bytes 221192 | tf_op jit(solution)/shard_map/ppermute | solution.py:428
  38.6 1.9 %collective-permute-start.8 = (f32[36,128]{1,0:T(8,128)S(1)}, f32[36,128]{1,0:T(8,128)S(1)}, u32[]{:S(2)}, u32[]{:S(2)}) collective-permute-start(f32[36,128]{1,0:T(8,128)S(1)} %get-tuple-element.50), channel_id=1, source_target_pairs={{0,4},{8,12},{16,20},{24,28},{4,0},{12,8},{20,16},{28,24},{1,5},{9... | collective-permute-start | bytes 55304 | tf_op jit(solution)/shard_map/ppermute | solution.py:433
  40.5 2.3 %collective-permute-start.9 = (f32[36,128]{1,0:T(8,128)S(1)}, f32[36,128]{1,0:T(8,128)S(1)}, u32[]{:S(2)}, u32[]{:S(2)}) collective-permute-start(f32[36,128]{1,0:T(8,128)S(1)} %get-tuple-element.51), channel_id=1, source_target_pairs={{4,8},{12,16},{20,24},{8,4},{16,12},{24,20},{5,9},{13,17},{21,25},... | collective-permute-start | bytes 55304 | tf_op jit(solution)/shard_map/ppermute | solution.py:433
  42.8 3.7 %collective-permute-start.10 = (f32[8,128]{1,0:T(8,128)S(1)}, f32[8,128]{1,0:T(8,128)S(1)}, u32[]{:S(2)}, u32[]{:S(2)}) collective-permute-start(f32[8,128]{1,0:T(8,128)S(1)} %get-tuple-element.52), channel_id=1, source_target_pairs={{0,1},{1,2},{2,3},{4,5},{5,6},{6,7},{8,9},{9,10},{10,11},{12,13},{... | collective-permute-start | bytes 12296 | tf_op jit(solution)/shard_map/ppermute | solution.py:428
  46.5 6.7 %collective-permute-done.10.zlo = f32[8,128]{1,0:T(8,128)S(1)} collective-permute-done((f32[8,128]{1,0:T(8,128)S(1)}, f32[8,128]{1,0:T(8,128)S(1)}, u32[]{:S(2)}, u32[]{:S(2)}) %collective-permute-start.10) | collective-permute-done | bytes 4128 | tf_op jit(solution)/shard_map/ppermute | solution.py:428
  53.2 1.9 %collective-permute-start.11 = (f32[8,128]{1,0:T(8,128)S(1)}, f32[8,128]{1,0:T(8,128)S(1)}, u32[]{:S(2)}, u32[]{:S(2)}) collective-permute-start(f32[8,128]{1,0:T(8,128)S(1)} %get-tuple-element.53), channel_id=1, source_target_pairs={{1,0},{2,1},{3,2},{5,4},{6,5},{7,6},{9,8},{10,9},{11,10},{13,12},{... | collective-permute-start | bytes 12296 | tf_op jit(solution)/shard_map/ppermute | solution.py:428
  55.1 3.6 %collective-permute-done.11.zhi = f32[8,128]{1,0:T(8,128)S(1)} collective-permute-done((f32[8,128]{1,0:T(8,128)S(1)}, f32[8,128]{1,0:T(8,128)S(1)}, u32[]{:S(2)}, u32[]{:S(2)}) %collective-permute-start.11) | collective-permute-done | bytes 4128 | tf_op jit(solution)/shard_map/ppermute | solution.py:428
  58.7 0.0 collective-permute-done.8.yeven
  58.7 0.0 collective-permute-done.9.yodd
  58.7 0.0 collective-permute-done.6.xlo
  58.7 0.0 collective-permute-done.7.xhi
  58.7 0.0 copy-done
  58.7 1.0 %diverge.1 = (f32[3,4,16,128]{3,2,1,0:T(8,128)}, f32[3,4,16,128]{3,2,1,0:T(8,128)}, f32[3,4,16,128]{3,2,1,0:T(8,128)}) custom-call(f32[18,4,16,128]{3,2,1,0:T(8,128)S(1)} %get-tuple-element.47.tensor_ref, f32[9,16,128]{2,1,0:T(8,128)S(1)} %collective-permute-done.6.xlo, f32[9,16,128]{2,1,0:T(8,128)S(1)} %collective-permute-done.7.xhi, ...), custom_call_target="tpu_custom_call" | custom-call | tf_op jit(solution)/shard_map/diverge/pallas_call | solution.py:517
Async XLA Ops:
  1.9 22.8 %collective-permute-start = (f32[9,16,128]{2,1,0:T(8,128)S(1)}, f32[9,16,128]{2,1,0:T(8,128)S(1)}, u32[]{:S(2)}, u32[]{:S(2)}) collective-permute-start(f32[9,16,128]{2,1,0:T(8,128)S(1)} %get-tuple-element.34), channel_id=1, source_target_pairs={{0,32},{32,64},{64,96},{96,128},{128,160},{160,192},{192,224},{224... | collective-permute-start | bytes 221192 | tf_op jit(solution)/shard_map/ppermute | solution.py:428
  4.8 19.8 %collective-permute-start.1 = (f32[9,16,128]{2,1,0:T(8,128)S(1)}, f32[9,16,128]{2,1,0:T(8,128)S(1)}, u32[]{:S(2)}, u32[]{:S(2)}) collective-permute-start(f32[9,16,128]{2,1,0:T(8,128)S(1)} %get-tuple-element.35), channel_id=1, source_target_pairs={{32,0},{64,32},{96,64},{128,96},{160,128},{192,160},{224,192},{256... | collective-permute-start | bytes 221192 | tf_op jit(solution)/shard_map/ppermute | solution.py:428
  8.9 15.7 %collective-permute-start.2 = (f32[36,128]{1,0:T(8,128)S(1)}, f32[36,128]{1,0:T(8,128)S(1)}, u32[]{:S(2)}, u32[]{:S(2)}) collective-permute-start(f32[36,128]{1,0:T(8,128)S(1)} %get-tuple-element.36), channel_id=1, source_target_pairs={{0,4},{8,12},{16,20},{24,28},{4,0},{12,8},{20,16},{28,24},{1,5},{9... | collective-permute-start | bytes 55304 | tf_op jit(solution)/shard_map/ppermute | solution.py:433
  10.9 13.8 %collective-permute-start.3 = (f32[36,128]{1,0:T(8,128)S(1)}, f32[36,128]{1,0:T(8,128)S(1)}, u32[]{:S(2)}, u32[]{:S(2)}) collective-permute-start(f32[36,128]{1,0:T(8,128)S(1)} %get-tuple-element.37), channel_id=1, source_target_pairs={{4,8},{12,16},{20,24},{8,4},{16,12},{24,20},{5,9},{13,17},{21,25},... | collective-permute-start | bytes 55304 | tf_op jit(solution)/shard_map/ppermute | solution.py:433
  13.6 5.5 %collective-permute-start.4 = (f32[8,128]{1,0:T(8,128)S(1)}, f32[8,128]{1,0:T(8,128)S(1)}, u32[]{:S(2)}, u32[]{:S(2)}) collective-permute-start(f32[8,128]{1,0:T(8,128)S(1)} %get-tuple-element.38), channel_id=1, source_target_pairs={{0,1},{1,2},{2,3},{4,5},{5,6},{6,7},{8,9},{9,10},{10,11},{12,13},{... | collective-permute-start | bytes 12296 | tf_op jit(solution)/shard_map/ppermute | solution.py:428
  19.1 5.5 %collective-permute-start.5 = (f32[8,128]{1,0:T(8,128)S(1)}, f32[8,128]{1,0:T(8,128)S(1)}, u32[]{:S(2)}, u32[]{:S(2)}) collective-permute-start(f32[8,128]{1,0:T(8,128)S(1)} %get-tuple-element.39), channel_id=1, source_target_pairs={{1,0},{2,1},{3,2},{5,4},{6,5},{7,6},{9,8},{10,9},{11,10},{13,12},{... | collective-permute-start | bytes 12296 | tf_op jit(solution)/shard_map/ppermute | solution.py:428
  24.6 34.0 %copy-start = (f32[3,4,16,128]{3,2,1,0:T(8,128)S(1)}, f32[3,4,16,128]{3,2,1,0:T(8,128)}, u32[]{:S(2)}) copy-start(f32[3,4,16,128]{3,2,1,0:T(8,128)} %force_ref.1) | copy-start | bytes 294916
  31.5 27.2 %collective-permute-start.6 = (f32[9,16,128]{2,1,0:T(8,128)S(1)}, f32[9,16,128]{2,1,0:T(8,128)S(1)}, u32[]{:S(2)}, u32[]{:S(2)}) collective-permute-start(f32[9,16,128]{2,1,0:T(8,128)S(1)} %get-tuple-element.48), channel_id=1, source_target_pairs={{0,32},{32,64},{64,96},{96,128},{128,160},{160,192},{192,224},{224... | collective-permute-start | bytes 221192 | tf_op jit(solution)/shard_map/ppermute | solution.py:428
  33.4 25.3 %collective-permute-start.7 = (f32[9,16,128]{2,1,0:T(8,128)S(1)}, f32[9,16,128]{2,1,0:T(8,128)S(1)}, u32[]{:S(2)}, u32[]{:S(2)}) collective-permute-start(f32[9,16,128]{2,1,0:T(8,128)S(1)} %get-tuple-element.49), channel_id=1, source_target_pairs={{32,0},{64,32},{96,64},{128,96},{160,128},{192,160},{224,192},{256... | collective-permute-start | bytes 221192 | tf_op jit(solution)/shard_map/ppermute | solution.py:428
  38.6 20.1 %collective-permute-start.8 = (f32[36,128]{1,0:T(8,128)S(1)}, f32[36,128]{1,0:T(8,128)S(1)}, u32[]{:S(2)}, u32[]{:S(2)}) collective-permute-start(f32[36,128]{1,0:T(8,128)S(1)} %get-tuple-element.50), channel_id=1, source_target_pairs={{0,4},{8,12},{16,20},{24,28},{4,0},{12,8},{20,16},{28,24},{1,5},{9... | collective-permute-start | bytes 55304 | tf_op jit(solution)/shard_map/ppermute | solution.py:433
  40.5 18.2 %collective-permute-start.9 = (f32[36,128]{1,0:T(8,128)S(1)}, f32[36,128]{1,0:T(8,128)S(1)}, u32[]{:S(2)}, u32[]{:S(2)}) collective-permute-start(f32[36,128]{1,0:T(8,128)S(1)} %get-tuple-element.51), channel_id=1, source_target_pairs={{4,8},{12,16},{20,24},{8,4},{16,12},{24,20},{5,9},{13,17},{21,25},... | collective-permute-start | bytes 55304 | tf_op jit(solution)/shard_map/ppermute | solution.py:433
  42.8 10.4 %collective-permute-start.10 = (f32[8,128]{1,0:T(8,128)S(1)}, f32[8,128]{1,0:T(8,128)S(1)}, u32[]{:S(2)}, u32[]{:S(2)}) collective-permute-start(f32[8,128]{1,0:T(8,128)S(1)} %get-tuple-element.52), channel_id=1, source_target_pairs={{0,1},{1,2},{2,3},{4,5},{5,6},{6,7},{8,9},{9,10},{10,11},{12,13},{... | collective-permute-start | bytes 12296 | tf_op jit(solution)/shard_map/ppermute | solution.py:428
  53.2 5.5 %collective-permute-start.11 = (f32[8,128]{1,0:T(8,128)S(1)}, f32[8,128]{1,0:T(8,128)S(1)}, u32[]{:S(2)}, u32[]{:S(2)}) collective-permute-start(f32[8,128]{1,0:T(8,128)S(1)} %get-tuple-element.53), channel_id=1, source_target_pairs={{1,0},{2,1},{3,2},{5,4},{6,5},{7,6},{9,8},{10,9},{11,10},{13,12},{... | collective-permute-start | bytes 12296 | tf_op jit(solution)/shard_map/ppermute | solution.py:428
where the time goes:
time: 60.2 us; the launch traced here: 59.7 us
  starting transfers between devices  33.9 us (56%)
  waiting for transfers between devices  13.9 us (23%)
  Pallas kernels  11.1 us (18%)
  between operations  0.79 us (1%)
    ppermute x8, starting transfers between devices, shift(): lax.ppermute(value, axis, [(i, i + step) for i in range(size) if 0 <= i +...  25 us
    ppermute x8, waiting for transfers between devices, shift(): lax.ppermute(value, axis, [(i, i + step) for i in range(size) if 0 <= i +...  13.9 us
    ppermute x4, starting transfers between devices, swap(): return lax.ppermute(value, axis, pairs + [(j, i) for i, j in pairs])  8.9 us
    pallas_call x1, Pallas kernels, on_device(): pl.pallas_call(material_kernel, out_shape=[shaped(SLIP, nx, ny, nz)] * 2...  6.83 us
    pallas_call x1, Pallas kernels, on_device(): pl.pallas_call(table_kernel, out_shape=[shaped(k, nx, ny, nz) for k in (l...  1.99 us
    pallas_call x1, Pallas kernels, on_device(): pl.pallas_call(faces_kernel, out_shape=[shaped(9, nx, ny, nz)] + [shape_o...  1.24 us
  transfers between devices with their start and end apart: 12, of which 4 were waited for; matrix products, arithmetic and copies ran while one was open for 0% of the time, Pallas kernels for 3%

commit v1 on v0

--- a/solution.py
+++ b/solution.py
@@ -52,10 +52,10 @@
     return acc
 
 
-def pack_lane(tiles, lane):
+def pack_lane(tiles, lane, slots=None, packed=None):
     at = lax.broadcasted_iota(jnp.int32, (8, LANES), 1)
-    packed = jnp.zeros((8, LANES), jnp.float32)
-    for k, tile in enumerate(tiles):
+    packed = jnp.zeros((8, LANES), jnp.float32) if packed is None else packed
+    for k, tile in zip(slots or range(len(tiles)), tiles):
         shift = (k - lane) % LANES
         moved = pltpu.roll(tile, shift, 1) if shift else tile
         packed = jnp.where(at == k, moved, packed)
@@ -265,6 +265,8 @@
     odd = parity()
     row_even, row_odd = (1 - odd) * (ny - 1), odd * (ny - 1)
     oxlo, oxhi, oyeven, oyodd, ozlo, ozhi = in_order((out0, out1, out2, out3, out4, out5), ORDER_LAST)
+    ozlo[...] = jnp.zeros_like(ozlo)
+    ozhi[...] = jnp.zeros_like(ozhi)
     tell = pltpu.make_async_copy(count_vmem, count_ref, told)
     tell.start()
     sort_halos(odd, yeven, yodd, ylo, yhi)
@@ -364,20 +366,22 @@
 
             tangent(1)
             tangent(2)
-    tiles = []
+            slots, tiles = [], []
+            for n in range(9):
+                for x in range(x0, x0 + WIDE):
+                    slots.append((n * nx + x) * (ny // 8) + h)
+                    tiles.append(tensor_out[6 * (n // 3) + SYM[n % 3][2], x, pl.ds(8 * h, 8), :])
+            ozlo[...] = pack_lane(tiles, 0, slots, ozlo[...])
+            ozhi[...] = pack_lane(tiles, LANES - 1, slots, ozhi[...])
     for f in range(3):
         for i in range(3):
             n = 3 * f + i
-            sx, sy, sz = (6 * f + SYM[i][j] for j in range(3))
+            sx, sy = (6 * f + SYM[i][j] for j in range(2))
             oxlo[n] = tensor_out[sx, 0]
             oxhi[n] = tensor_out[sx, nx - 1]
             for x in range(nx):
                 oyeven[pl.ds(n * nx + x, 1), :] = tensor_out[sy, x, pl.ds(row_even, 1), :]
                 oyodd[pl.ds(n * nx + x, 1), :] = tensor_out[sy, x, pl.ds(row_odd, 1), :]
-                for h in range(ny // 8):
-                    tiles.append(tensor_out[sz, x, pl.ds(8 * h, 8), :])
-    ozlo[...] = pack_lane(tiles, 0)
-    ozhi[...] = pack_lane(tiles, LANES - 1)
     for copy in copies:
         copy.wait()
 

time: 60.2 us -> 60.4 us (level)
  no operation moved by 1% of the time
where the time goes in v1:
time: 60.4 us; the launch traced here: 59.9 us
  starting transfers between devices  33.9 us (56%)
  waiting for transfers between devices  14 us (23%)
  Pallas kernels  11.2 us (19%)
  between operations  0.79 us (1%)
    ppermute x8, starting transfers between devices, shift(): lax.ppermute(value, axis, [(i, i + step) for i in range(size) if 0 <= i +...  25 us
    ppermute x8, waiting for transfers between devices, shift(): lax.ppermute(value, axis, [(i, i + step) for i in range(size) if 0 <= i +...  13.9 us
    ppermute x4, starting transfers between devices, swap(): return lax.ppermute(value, axis, pairs + [(j, i) for i, j in pairs])  8.9 us
    pallas_call x1, Pallas kernels, on_device(): pl.pallas_call(material_kernel, out_shape=[shaped(SLIP, nx, ny, nz)] * 2...  6.97 us
    pallas_call x1, Pallas kernels, on_device(): pl.pallas_call(table_kernel, out_shape=[shaped(k, nx, ny, nz) for k in (l...  1.99 us
    pallas_call x1, Pallas kernels, on_device(): pl.pallas_call(faces_kernel, out_shape=[shaped(9, nx, ny, nz)] + [shape_o...  1.24 us
  transfers between devices with their start and end apart: 12, of which 4 were waited for; matrix products, arithmetic and copies ran while one was open for 0% of the time, Pallas kernels for 3%

profile of v1, /device:TPU:282, one launch (start us, length us, event | category | flops | bytes accessed | tf_op | source)
XLA Modules:
  0.0 59.9 jit_solution(10324758533674380765)
XLA Ops:
  0.6 1.2 %faces.1 = (f32[9,4,16,128]{3,2,1,0:T(8,128)S(1)}, f32[9,16,128]{2,1,0:T(8,128)S(1)}, f32[9,16,128]{2,1,0:T(8,128)S(1)}, f32[36,128]{1,0:T(8,128)S(1)}, f32[36,1...) custom-call(f32[3,4,16,128]{3,2,1,0:T(8,128)} %u_hbm.1, f32[3,4,16,128]{3,2,1,0:T(8,128)} %a_hbm.1, ...), custom_call_target="tpu_custom_call" | custom-call | tf_op jit(solution)/shard_map/faces/pallas_call | solution.py:468
  1.9 2.9 %collective-permute-start = (f32[9,16,128]{2,1,0:T(8,128)S(1)}, f32[9,16,128]{2,1,0:T(8,128)S(1)}, u32[]{:S(2)}, u32[]{:S(2)}) collective-permute-start(f32[9,16,128]{2,1,0:T(8,128)S(1)} %get-tuple-element.34), channel_id=1, source_target_pairs={{0,32},{32,64},{64,96},{96,128},{128,160},{160,192},{192,224},{224... | collective-permute-start | bytes 221192 | tf_op jit(solution)/shard_map/ppermute | solution.py:432
  4.8 4.1 %collective-permute-start.1 = (f32[9,16,128]{2,1,0:T(8,128)S(1)}, f32[9,16,128]{2,1,0:T(8,128)S(1)}, u32[]{:S(2)}, u32[]{:S(2)}) collective-permute-start(f32[9,16,128]{2,1,0:T(8,128)S(1)} %get-tuple-element.35), channel_id=1, source_target_pairs={{32,0},{64,32},{96,64},{128,96},{160,128},{192,160},{224,192},{256... | collective-permute-start | bytes 221192 | tf_op jit(solution)/shard_map/ppermute | solution.py:432
  8.9 1.9 %collective-permute-start.2 = (f32[36,128]{1,0:T(8,128)S(1)}, f32[36,128]{1,0:T(8,128)S(1)}, u32[]{:S(2)}, u32[]{:S(2)}) collective-permute-start(f32[36,128]{1,0:T(8,128)S(1)} %get-tuple-element.36), channel_id=1, source_target_pairs={{0,4},{8,12},{16,20},{24,28},{4,0},{12,8},{20,16},{28,24},{1,5},{9... | collective-permute-start | bytes 55304 | tf_op jit(solution)/shard_map/ppermute | solution.py:437
  10.9 2.8 %collective-permute-start.3 = (f32[36,128]{1,0:T(8,128)S(1)}, f32[36,128]{1,0:T(8,128)S(1)}, u32[]{:S(2)}, u32[]{:S(2)}) collective-permute-start(f32[36,128]{1,0:T(8,128)S(1)} %get-tuple-element.37), channel_id=1, source_target_pairs={{4,8},{12,16},{20,24},{8,4},{16,12},{24,20},{5,9},{13,17},{21,25},... | collective-permute-start | bytes 55304 | tf_op jit(solution)/shard_map/ppermute | solution.py:437
  13.6 3.4 %collective-permute-start.4 = (f32[8,128]{1,0:T(8,128)S(1)}, f32[8,128]{1,0:T(8,128)S(1)}, u32[]{:S(2)}, u32[]{:S(2)}) collective-permute-start(f32[8,128]{1,0:T(8,128)S(1)} %get-tuple-element.38), channel_id=1, source_target_pairs={{0,1},{1,2},{2,3},{4,5},{5,6},{6,7},{8,9},{9,10},{10,11},{12,13},{... | collective-permute-start | bytes 12296 | tf_op jit(solution)/shard_map/ppermute | solution.py:432
  17.0 2.1 %collective-permute-done.4.zlo = f32[8,128]{1,0:T(8,128)S(1)} collective-permute-done((f32[8,128]{1,0:T(8,128)S(1)}, f32[8,128]{1,0:T(8,128)S(1)}, u32[]{:S(2)}, u32[]{:S(2)}) %collective-permute-start.4) | collective-permute-done | bytes 4128 | tf_op jit(solution)/shard_map/ppermute | solution.py:432
  19.1 1.9 %collective-permute-start.5 = (f32[8,128]{1,0:T(8,128)S(1)}, f32[8,128]{1,0:T(8,128)S(1)}, u32[]{:S(2)}, u32[]{:S(2)}) collective-permute-start(f32[8,128]{1,0:T(8,128)S(1)} %get-tuple-element.39), channel_id=1, source_target_pairs={{1,0},{2,1},{3,2},{5,4},{6,5},{7,6},{9,8},{10,9},{11,10},{13,12},{... | collective-permute-start | bytes 12296 | tf_op jit(solution)/shard_map/ppermute | solution.py:432
  21.1 2.0 %table.1 = (f32[50,4,16,128]{3,2,1,0:T(8,128)S(1)}, f32[25,4,16,128]{3,2,1,0:T(8,128)S(1)}, f32[5,4,16,128]{3,2,1,0:T(8,128)S(1)}, s32[4,16,128]{2,1,0:T(8,128)S...) custom-call(f32[9,12,64]{2,1,0:T(8,128)} %bitcast.4, ...), custom_call_target="tpu_custom_call" | custom-call | tf_op jit(solution)/shard_map/table/pallas_call | solution.py:479
  23.0 1.6 %collective-permute-done.5.zhi = f32[8,128]{1,0:T(8,128)S(1)} collective-permute-done((f32[8,128]{1,0:T(8,128)S(1)}, f32[8,128]{1,0:T(8,128)S(1)}, u32[]{:S(2)}, u32[]{:S(2)}) %collective-permute-start.5) | collective-permute-done | bytes 4128 | tf_op jit(solution)/shard_map/ppermute | solution.py:432
  24.6 0.0 collective-permute-done.2.yeven
  24.6 0.0 collective-permute-done.3.yodd
  24.6 0.0 collective-permute-done.xlo
  24.6 0.0 collective-permute-done.1.xhi
  24.6 0.0 copy-start
  24.7 7.0 %material.1 = (f32[12,4,16,128]{3,2,1,0:T(8,128)}, f32[12,4,16,128]{3,2,1,0:T(8,128)}, f32[18,4,16,128]{3,2,1,0:T(8,128)S(1)}, f32[36,128]{1,0:T(8,128)S(1)}, f3...) custom-call(s32[4,1,8]{2,1,0:T(1,128)S(1)} %get-tuple-element.32.cou, ...), custom_call_target="tpu_custom_call" | custom-call | tf_op jit(solution)/shard_map/material/pallas_call | solution.py:498
  31.6 1.9 %collective-permute-start.6 = (f32[9,16,128]{2,1,0:T(8,128)S(1)}, f32[9,16,128]{2,1,0:T(8,128)S(1)}, u32[]{:S(2)}, u32[]{:S(2)}) collective-permute-start(f32[9,16,128]{2,1,0:T(8,128)S(1)} %get-tuple-element.48), channel_id=1, source_target_pairs={{0,32},{32,64},{64,96},{96,128},{128,160},{160,192},{192,224},{224... | collective-permute-start | bytes 221192 | tf_op jit(solution)/shard_map/ppermute | solution.py:432
  33.6 5.1 %collective-permute-start.7 = (f32[9,16,128]{2,1,0:T(8,128)S(1)}, f32[9,16,128]{2,1,0:T(8,128)S(1)}, u32[]{:S(2)}, u32[]{:S(2)}) collective-permute-start(f32[9,16,128]{2,1,0:T(8,128)S(1)} %get-tuple-element.49), channel_id=1, source_target_pairs={{32,0},{64,32},{96,64},{128,96},{160,128},{192,160},{224,192},{256... | collective-permute-start | bytes 221192 | tf_op jit(solution)/shard_map/ppermute | solution.py:432
  38.7 1.9 %collective-permute-start.8 = (f32[36,128]{1,0:T(8,128)S(1)}, f32[36,128]{1,0:T(8,128)S(1)}, u32[]{:S(2)}, u32[]{:S(2)}) collective-permute-start(f32[36,128]{1,0:T(8,128)S(1)} %get-tuple-element.50), channel_id=1, source_target_pairs={{0,4},{8,12},{16,20},{24,28},{4,0},{12,8},{20,16},{28,24},{1,5},{9... | collective-permute-start | bytes 55304 | tf_op jit(solution)/shard_map/ppermute | solution.py:437
  40.6 2.3 %collective-permute-start.9 = (f32[36,128]{1,0:T(8,128)S(1)}, f32[36,128]{1,0:T(8,128)S(1)}, u32[]{:S(2)}, u32[]{:S(2)}) collective-permute-start(f32[36,128]{1,0:T(8,128)S(1)} %get-tuple-element.51), channel_id=1, source_target_pairs={{4,8},{12,16},{20,24},{8,4},{16,12},{24,20},{5,9},{13,17},{21,25},... | collective-permute-start | bytes 55304 | tf_op jit(solution)/shard_map/ppermute | solution.py:437
  43.0 3.7 %collective-permute-start.10 = (f32[8,128]{1,0:T(8,128)S(1)}, f32[8,128]{1,0:T(8,128)S(1)}, u32[]{:S(2)}, u32[]{:S(2)}) collective-permute-start(f32[8,128]{1,0:T(8,128)S(1)} %get-tuple-element.52), channel_id=1, source_target_pairs={{0,1},{1,2},{2,3},{4,5},{5,6},{6,7},{8,9},{9,10},{10,11},{12,13},{... | collective-permute-start | bytes 12296 | tf_op jit(solution)/shard_map/ppermute | solution.py:432
  46.7 6.7 %collective-permute-done.10.zlo = f32[8,128]{1,0:T(8,128)S(1)} collective-permute-done((f32[8,128]{1,0:T(8,128)S(1)}, f32[8,128]{1,0:T(8,128)S(1)}, u32[]{:S(2)}, u32[]{:S(2)}) %collective-permute-start.10) | collective-permute-done | bytes 4128 | tf_op jit(solution)/shard_map/ppermute | solution.py:432
  53.4 1.9 %collective-permute-start.11 = (f32[8,128]{1,0:T(8,128)S(1)}, f32[8,128]{1,0:T(8,128)S(1)}, u32[]{:S(2)}, u32[]{:S(2)}) collective-permute-start(f32[8,128]{1,0:T(8,128)S(1)} %get-tuple-element.53), channel_id=1, source_target_pairs={{1,0},{2,1},{3,2},{5,4},{6,5},{7,6},{9,8},{10,9},{11,10},{13,12},{... | collective-permute-start | bytes 12296 | tf_op jit(solution)/shard_map/ppermute | solution.py:432
  55.3 3.6 %collective-permute-done.11.zhi = f32[8,128]{1,0:T(8,128)S(1)} collective-permute-done((f32[8,128]{1,0:T(8,128)S(1)}, f32[8,128]{1,0:T(8,128)S(1)}, u32[]{:S(2)}, u32[]{:S(2)}) %collective-permute-start.11) | collective-permute-done | bytes 4128 | tf_op jit(solution)/shard_map/ppermute | solution.py:432
  58.9 0.0 collective-permute-done.8.yeven
  58.9 0.0 collective-permute-done.9.yodd
  58.9 0.0 collective-permute-done.6.xlo
  58.9 0.0 collective-permute-done.7.xhi
  58.9 0.0 copy-done
  58.9 1.0 %diverge.1 = (f32[3,4,16,128]{3,2,1,0:T(8,128)}, f32[3,4,16,128]{3,2,1,0:T(8,128)}, f32[3,4,16,128]{3,2,1,0:T(8,128)}) custom-call(f32[18,4,16,128]{3,2,1,0:T(8,128)S(1)} %get-tuple-element.47.tensor_ref, f32[9,16,128]{2,1,0:T(8,128)S(1)} %collective-permute-done.6.xlo, f32[9,16,128]{2,1,0:T(8,128)S(1)} %collective-permute-done.7.xhi, ...), custom_call_target="tpu_custom_call" | custom-call | tf_op jit(solution)/shard_map/diverge/pallas_call | solution.py:521
Async XLA Ops:
  1.9 22.8 %collective-permute-start = (f32[9,16,128]{2,1,0:T(8,128)S(1)}, f32[9,16,128]{2,1,0:T(8,128)S(1)}, u32[]{:S(2)}, u32[]{:S(2)}) collective-permute-start(f32[9,16,128]{2,1,0:T(8,128)S(1)} %get-tuple-element.34), channel_id=1, source_target_pairs={{0,32},{32,64},{64,96},{96,128},{128,160},{160,192},{192,224},{224... | collective-permute-start | bytes 221192 | tf_op jit(solution)/shard_map/ppermute | solution.py:432
  4.8 19.8 %collective-permute-start.1 = (f32[9,16,128]{2,1,0:T(8,128)S(1)}, f32[9,16,128]{2,1,0:T(8,128)S(1)}, u32[]{:S(2)}, u32[]{:S(2)}) collective-permute-start(f32[9,16,128]{2,1,0:T(8,128)S(1)} %get-tuple-element.35), channel_id=1, source_target_pairs={{32,0},{64,32},{96,64},{128,96},{160,128},{192,160},{224,192},{256... | collective-permute-start | bytes 221192 | tf_op jit(solution)/shard_map/ppermute | solution.py:432
  8.9 15.7 %collective-permute-start.2 = (f32[36,128]{1,0:T(8,128)S(1)}, f32[36,128]{1,0:T(8,128)S(1)}, u32[]{:S(2)}, u32[]{:S(2)}) collective-permute-start(f32[36,128]{1,0:T(8,128)S(1)} %get-tuple-element.36), channel_id=1, source_target_pairs={{0,4},{8,12},{16,20},{24,28},{4,0},{12,8},{20,16},{28,24},{1,5},{9... | collective-permute-start | bytes 55304 | tf_op jit(solution)/shard_map/ppermute | solution.py:437
  10.9 13.8 %collective-permute-start.3 = (f32[36,128]{1,0:T(8,128)S(1)}, f32[36,128]{1,0:T(8,128)S(1)}, u32[]{:S(2)}, u32[]{:S(2)}) collective-permute-start(f32[36,128]{1,0:T(8,128)S(1)} %get-tuple-element.37), channel_id=1, source_target_pairs={{4,8},{12,16},{20,24},{8,4},{16,12},{24,20},{5,9},{13,17},{21,25},... | collective-permute-start | bytes 55304 | tf_op jit(solution)/shard_map/ppermute | solution.py:437
  13.6 5.5 %collective-permute-start.4 = (f32[8,128]{1,0:T(8,128)S(1)}, f32[8,128]{1,0:T(8,128)S(1)}, u32[]{:S(2)}, u32[]{:S(2)}) collective-permute-start(f32[8,128]{1,0:T(8,128)S(1)} %get-tuple-element.38), channel_id=1, source_target_pairs={{0,1},{1,2},{2,3},{4,5},{5,6},{6,7},{8,9},{9,10},{10,11},{12,13},{... | collective-permute-start | bytes 12296 | tf_op jit(solution)/shard_map/ppermute | solution.py:432
  19.1 5.5 %collective-permute-start.5 = (f32[8,128]{1,0:T(8,128)S(1)}, f32[8,128]{1,0:T(8,128)S(1)}, u32[]{:S(2)}, u32[]{:S(2)}) collective-permute-start(f32[8,128]{1,0:T(8,128)S(1)} %get-tuple-element.39), channel_id=1, source_target_pairs={{1,0},{2,1},{3,2},{5,4},{6,5},{7,6},{9,8},{10,9},{11,10},{13,12},{... | collective-permute-start | bytes 12296 | tf_op jit(solution)/shard_map/ppermute | solution.py:432
  24.6 34.2 %copy-start = (f32[3,4,16,128]{3,2,1,0:T(8,128)S(1)}, f32[3,4,16,128]{3,2,1,0:T(8,128)}, u32[]{:S(2)}) copy-start(f32[3,4,16,128]{3,2,1,0:T(8,128)} %force_ref.1) | copy-start | bytes 294916
  31.6 27.2 %collective-permute-start.6 = (f32[9,16,128]{2,1,0:T(8,128)S(1)}, f32[9,16,128]{2,1,0:T(8,128)S(1)}, u32[]{:S(2)}, u32[]{:S(2)}) collective-permute-start(f32[9,16,128]{2,1,0:T(8,128)S(1)} %get-tuple-element.48), channel_id=1, source_target_pairs={{0,32},{32,64},{64,96},{96,128},{128,160},{160,192},{192,224},{224... | collective-permute-start | bytes 221192 | tf_op jit(solution)/shard_map/ppermute | solution.py:432
  33.6 25.3 %collective-permute-start.7 = (f32[9,16,128]{2,1,0:T(8,128)S(1)}, f32[9,16,128]{2,1,0:T(8,128)S(1)}, u32[]{:S(2)}, u32[]{:S(2)}) collective-permute-start(f32[9,16,128]{2,1,0:T(8,128)S(1)} %get-tuple-element.49), channel_id=1, source_target_pairs={{32,0},{64,32},{96,64},{128,96},{160,128},{192,160},{224,192},{256... | collective-permute-start | bytes 221192 | tf_op jit(solution)/shard_map/ppermute | solution.py:432
  38.7 20.1 %collective-permute-start.8 = (f32[36,128]{1,0:T(8,128)S(1)}, f32[36,128]{1,0:T(8,128)S(1)}, u32[]{:S(2)}, u32[]{:S(2)}) collective-permute-start(f32[36,128]{1,0:T(8,128)S(1)} %get-tuple-element.50), channel_id=1, source_target_pairs={{0,4},{8,12},{16,20},{24,28},{4,0},{12,8},{20,16},{28,24},{1,5},{9... | collective-permute-start | bytes 55304 | tf_op jit(solution)/shard_map/ppermute | solution.py:437
  40.6 18.2 %collective-permute-start.9 = (f32[36,128]{1,0:T(8,128)S(1)}, f32[36,128]{1,0:T(8,128)S(1)}, u32[]{:S(2)}, u32[]{:S(2)}) collective-permute-start(f32[36,128]{1,0:T(8,128)S(1)} %get-tuple-element.51), channel_id=1, source_target_pairs={{4,8},{12,16},{20,24},{8,4},{16,12},{24,20},{5,9},{13,17},{21,25},... | collective-permute-start | bytes 55304 | tf_op jit(solution)/shard_map/ppermute | solution.py:437
  43.0 10.4 %collective-permute-start.10 = (f32[8,128]{1,0:T(8,128)S(1)}, f32[8,128]{1,0:T(8,128)S(1)}, u32[]{:S(2)}, u32[]{:S(2)}) collective-permute-start(f32[8,128]{1,0:T(8,128)S(1)} %get-tuple-element.52), channel_id=1, source_target_pairs={{0,1},{1,2},{2,3},{4,5},{5,6},{6,7},{8,9},{9,10},{10,11},{12,13},{... | collective-permute-start | bytes 12296 | tf_op jit(solution)/shard_map/ppermute | solution.py:432
  53.4 5.5 %collective-permute-start.11 = (f32[8,128]{1,0:T(8,128)S(1)}, f32[8,128]{1,0:T(8,128)S(1)}, u32[]{:S(2)}, u32[]{:S(2)}) collective-permute-start(f32[8,128]{1,0:T(8,128)S(1)} %get-tuple-element.53), channel_id=1, source_target_pairs={{1,0},{2,1},{3,2},{5,4},{6,5},{7,6},{9,8},{10,9},{11,10},{13,12},{... | collective-permute-start | bytes 12296 | tf_op jit(solution)/shard_map/ppermute | solution.py:432
